TPU v7x, 32 devices: a whole 2x2x4 slice. The times are simulated.
32 devices in a mesh: cfg: 2 (over core), tp: 8 (over z, x), dp: 2 (over y).
Axes of the slice: x: 2, y: 2, z: 4, core: 2. Of those that a mesh axis runs over, the one named last changes fastest.
Arguments:
- tokens: bfloat16 [4096, 512], P('dp'), parts along dimension 0, may hold values from -6 to 6
- conditions: float32 [4, 256], P(('dp', 'cfg')), parts along dimension 0, may hold values from -6 to 6
- ada_block: bfloat16 [256, 3072], P(None, 'tp'), may hold values from -1 to 1
- ada_final: bfloat16 [256, 1024], P(None, 'tp'), may hold values from -1 to 1
- qkv_weight: bfloat16 [512, 3, 512], P(None, None, 'tp'), may hold values from -0.25 to 0.25
- out_weight: bfloat16 [512, 512], P('tp'), may hold values from -0.25 to 0.25
- up_weight: bfloat16 [512, 2048], P(None, 'tp'), may hold values from -0.25 to 0.25
- down_weight: bfloat16 [2048, 512], P('tp'), may hold values from -0.125 to 0.125
- final_weight: bfloat16 [512, 64], replicated, may hold values from -0.25 to 0.25
Outputs:
- guided: float32 [4096, 64], P('dp'), parts along dimension 0
There are 2 independent parts, one for each index of `dp`. A program takes and returns all parts, laid end to end along the dimension named above; an argument that names none is the same for every part. Nothing has to cross between parts.
All inputs are finite; a program needn't handle non-finite values.
Results may differ from a plain program's by a relative error of at most 0.02.
Values may be sent and summed in bfloat16 or wider, within the bound.
A program may use at most 128 MiB of HBM per device.

v0:
```python
import jax
import jax.numpy as jnp
from jax import lax
from jax.sharding import PartitionSpec as P

HEAD_SIZE = 64
guidance = 4.0
epsilon = 1e-06


def layer_norm(values):
    average = jnp.mean(values, -1, keepdims=True)
    centred = values - average
    spread = jnp.mean(centred * centred, -1, keepdims=True)
    return centred * lax.rsqrt(spread + epsilon)


def modulate(stream, scales, shifts):
    return (layer_norm(stream) * (1.0 + scales) + shifts).astype(jnp.bfloat16)


def attend(projected):
    token_count = projected.shape[0]
    local_width = projected.shape[2]
    local_heads = local_width // HEAD_SIZE
    per_head = projected.reshape(token_count, 3, local_heads, HEAD_SIZE)
    scores = jnp.einsum(
        "thd,shd->hts", per_head[:, 0], per_head[:, 1], preferred_element_type=jnp.float32
    ) * HEAD_SIZE ** (-0.5)
    softmaxed = jax.nn.softmax(scores, axis=-1)
    values_f = per_head[:, 2].astype(jnp.float32)
    head_out = jnp.einsum("hts,shd->thd", softmaxed, values_f)
    return head_out.reshape(token_count, local_width).astype(jnp.bfloat16)


def local(
    tokens,
    conditions,
    ada_block,
    ada_final,
    qkv_weight,
    out_weight,
    up_weight,
    down_weight,
    final_weight,
):
    model_width = tokens.shape[1]
    signal = jax.nn.silu(conditions).astype(jnp.bfloat16)
    block_local = jnp.dot(signal, ada_block, preferred_element_type=jnp.float32)[0]
    final_local = jnp.dot(signal, ada_final, preferred_element_type=jnp.float32)[0]
    shifts, final_mod = (
        lax.all_gather(block_local, "tp", axis=0, tiled=True),
        lax.all_gather(final_local, "tp", axis=0, tiled=True),
    )
    shifts = shifts.reshape(6, model_width)
    stream = tokens.astype(jnp.float32)
    normed = modulate(stream, shifts[1], shifts[0])
    projected = jnp.einsum(
        "td,dke->tke", normed, qkv_weight, preferred_element_type=jnp.float32
    ).astype(jnp.bfloat16)
    head_out = attend(projected)
    attended = lax.psum(
        jnp.dot(head_out, out_weight, preferred_element_type=jnp.float32).astype(jnp.bfloat16), "tp"
    ).astype(jnp.float32)
    stream = stream + shifts[2] * attended
    normed = modulate(stream, shifts[4], shifts[3])
    upward = jnp.dot(normed, up_weight, preferred_element_type=jnp.float32)
    hidden = jax.nn.gelu(upward, approximate=True).astype(jnp.bfloat16)
    mlp_out = lax.psum(
        jnp.dot(hidden, down_weight, preferred_element_type=jnp.float32).astype(jnp.bfloat16), "tp"
    ).astype(jnp.float32)
    stream = stream + shifts[5] * mlp_out
    final_mod = final_mod.reshape(2, model_width)
    final_in = modulate(stream, final_mod[1], final_mod[0])
    predicted = jnp.dot(final_in, final_weight, preferred_element_type=jnp.float32)
    is_cond = lax.axis_index("cfg") == 0
    weighting = jnp.where(is_cond, guidance, 1.0 - guidance).astype(jnp.float32)
    return lax.psum((weighting * predicted).astype(jnp.bfloat16), "cfg").astype(jnp.float32)


def solution(mesh):
    placed = (
        P("dp", None),
        P(("dp", "cfg"), None),
        P(None, "tp"),
        P(None, "tp"),
        P(None, None, "tp"),
        P("tp", None),
        P(None, "tp"),
        P("tp", None),
        P(),
    )
    return jax.shard_map(
        local, mesh=mesh, in_specs=placed, out_specs=P("dp", None), check_vma=False
    )
```

profile of v0, /device:TPU:0, one launch (start us, length us, event | category | flops | bytes accessed | tf_op | source)
XLA Modules:
  0.0 313.4 jit_solution(2466030839063625285)
XLA Ops:
  6.5 0.0 copy-start
  6.5 0.0 copy-start.1
  6.5 0.0 copy-start.8
  6.5 0.0 all-reduce.4.cloned.1.call-start
  6.5 1.2 convolution_bitcast_fusion
  7.8 27.8 %all-gather = f32[8,1,384]{2,1,0:T(1,128)S(1)} all-gather(f32[1,1,384]{2,1,0:T(1,128)S(1)} %convolution_bitcast_fusion), channel_id=1, replica_groups=mesh['cfg'=2,'tp'=8,'dp'=2] {'tp'}, dimensions={0}, use_global_device_ids=true | all-gather | bytes 13824 | tf_op jit(solution)/shard_map/all_gather | solution.py:52
  35.6 1.9 convert_reduce_fusion
  37.6 2.5 fusion.8
  40.1 0.0 copy-done.1
  40.1 0.0 copy-done.8
  40.1 1.2 fusion.28
  41.3 0.1 convert_bitcast_fusion
  41.4 8.1 %multiply_reduce_fusion = (f32[2048]{0:T(1024)S(1)}, f32[2048,2048]{0,1:T(8,128)}) fusion(bf16[2048,3,1,64]{0,3,1,2:T(8,128)(2,1)S(1)} %convert_bitcast_fusion), kind=kOutput, calls=%fused_computation.3 | convolution fusion | flops 545257472 | bytes 17309696 | tf_op jit(solution)/shard_map/thd,shd->hts/dot_general | solution.py:27
  49.5 0.0 copy-start.9
  49.5 8.6 %fusion.2 = f32[2048]{0:T(1024)S(1)} fusion(f32[2048,2048]{0,1:T(8,128)} %get-tuple-element.14, f32[2048]{0:T(1024)S(1)} %get-tuple-element.13), kind=kLoop, calls=%fused_computation.4 | loop fusion | flops 12580864 | bytes 16793600 | tf_op jit(solution)/shard_map/reduce_sum | solution.py:30
  58.1 0.0 copy-done.9
  58.1 8.9 %convolution_convert_fusion.1 = bf16[2048,512]{1,0:T(8,128)(2,1)} fusion(bf16[64,512]{1,0:T(8,128)(2,1)S(1)} %copy-done.9, f32[2048,2048]{0,1:T(8,128)} %get-tuple-element.14, f32[2048]{0:T(1024)S(1)} %fusion.2, f32[2048]{0:T(1024)S(1)} %get-tuple-element.13, bf16[2048,3,1,64]{0,3,1,2:T(8,128)(2,1)S(1)} %convert_bitcast_fusion), kind=kOutput, calls=%fused_computation.24 | convolution fusion | flops 684851200 | bytes 19218432 | tf_op jit(solution)/shard_map/dot_general | solution.py:63
  67.0 0.0 all-reduce.4.cloned.1.call-update
  67.0 0.2 all-reduce.6.cloned.1.call-start
  67.3 101.6 %all-reduce.4.cloned.1.call-done = bf16[2048,512]{1,0:T(8,128)(2,1)} async-done(((bf16[2048,512]{1,0:T(8,128)(2,1)}), bf16[2048,512]{1,0:T(8,128)(2,1)}) %all-reduce.4.cloned.1.call-update) | async-done | bytes 2097168 | tf_op jit(solution)/shard_map/psum | solution.py:62
  168.9 0.0 copy-start.2
  168.9 0.0 copy-start.7
  168.9 2.5 fusion.12
  171.4 0.0 copy-done.2
  171.4 1.2 multiply_reduce_fusion.2
  172.6 0.0 copy-done
  172.6 0.0 copy-done.7
  172.6 0.0 copy-start.5
  172.6 0.0 copy-start.6
  172.6 5.1 %convolution_convert_fusion = bf16[2048,512]{1,0:T(8,128)(2,1)} fusion(bf16[256,512]{1,0:T(8,128)(2,1)S(1)} %copy-done, bf16[512,256]{1,0:T(8,128)(2,1)S(1)} %copy-done.7, bf16[2048,512]{1,0:T(8,128)(2,1)} %all-reduce.4.cloned.1.call-done, bf16[2048,512]{1,0:T(8,128)(2,1)S(1)} %copy-done.1, f32[512]{0:T(512)S(1)} %get-tuple-element.6, ...), kind=kOutput, calls=%fused_computation.23 | convolution fusion | flops 1088946176 | bytes 6838272 | tf_op jit(solution)/shard_map/dot_general | solution.py:70
  177.7 0.0 all-reduce.6.cloned.1.call-update
  177.8 0.0 all-reduce.8.cloned.1.call-start
  177.8 0.0 copy-done.5
  177.8 0.0 copy-done.6
  177.9 0.1 convolution_bitcast_fusion.1
  178.0 19.2 %all-gather.1 = f32[8,1,128]{2,1,0:T(1,128)S(1)} all-gather(f32[1,1,128]{2,1,0:T(1,128)S(1)} %convolution_bitcast_fusion.1), channel_id=1, replica_groups=mesh['cfg'=2,'tp'=8,'dp'=2] {'tp'}, dimensions={0}, use_global_device_ids=true | all-gather | bytes 4608 | tf_op jit(solution)/shard_map/all_gather | solution.py:53
  197.2 82.3 %all-reduce.6.cloned.1.call-done = bf16[2048,512]{1,0:T(8,128)(2,1)} async-done(((bf16[2048,512]{1,0:T(8,128)(2,1)}), bf16[2048,512]{1,0:T(8,128)(2,1)}) %all-reduce.6.cloned.1.call-update) | async-done | bytes 2097168 | tf_op jit(solution)/shard_map/psum | solution.py:69
  279.5 0.0 copy-start.3
  279.5 3.5 %fusion.45 = f32[2048]{0:T(1024)S(1)} fusion(bf16[2048,512]{1,0:T(8,128)(2,1)} %all-reduce.6.cloned.1.call-done, f32[512]{0:T(512)S(1)} %get-tuple-element.5, bf16[2048,512]{1,0:T(8,128)(2,1)} %all-reduce.4.cloned.1.call-done, f32[512]{0:T(512)S(1)} %get-tuple-element.10, bf16[2048,512]{1,0:T(8,128)(2,1)S(1)} %copy-done.1), kind=kLoop, calls=%fused_computation.58 | loop fusion | flops 8386560 | bytes 6303744 | tf_op jit(solution)/shard_map/reduce_sum | solution.py:12
  283.1 0.0 copy-start.10
  283.1 0.0 copy-done.3
  283.1 0.0 copy-done.4
  283.1 1.6 multiply_reduce_fusion.1
  284.7 0.0 copy-done.10
  284.7 2.7 fusion.13
  287.4 0.0 all-reduce.8.cloned.1.call-update
  287.4 17.7 %all-reduce.8.cloned.1.call-done = bf16[2048,64]{0,1:T(8,128)(2,1)} async-done(((bf16[2048,64]{0,1:T(8,128)(2,1)}), bf16[2048,64]{0,1:T(8,128)(2,1)}) %all-reduce.8.cloned.1.call-update) | async-done | bytes 262160 | tf_op jit(solution)/shard_map/psum | solution.py:78
  305.1 1.8 convert_element_type.68
  (9 shorter events, 0.0 us)
Async XLA Ops:
  6.5 166.1 %copy-start = (bf16[256,512]{1,0:T(8,128)(2,1)S(1)}, bf16[256,512]{1,0:T(8,128)(2,1)}, u32[]{:S(2)}) copy-start(bf16[256,512]{1,0:T(8,128)(2,1)} %param.16) | copy-start | bytes 786436
  6.5 33.5 %copy-start.1 = (bf16[2048,512]{1,0:T(8,128)(2,1)S(1)}, bf16[2048,512]{1,0:T(8,128)(2,1)}, u32[]{:S(2)}) copy-start(bf16[2048,512]{1,0:T(8,128)(2,1)} %param.9) | copy-start | bytes 6291460
  6.5 33.6 %copy-start.8 = (bf16[512,3,64]{0,2,1:T(8,128)(2,1)S(1)}, bf16[512,3,64]{0,2,1:T(8,128)(2,1)}, u32[]{:S(2)}) copy-start(bf16[512,3,64]{0,2,1:T(8,128)(2,1)} %param.13) | copy-start | bytes 589828
  6.5 162.3 %all-reduce.4.cloned.1.call-start = ((), (), s32[]{:S(2)}) async-start(), calls=%async_computation | async-start | bytes 4194304 | tf_op jit(solution)/shard_map/psum | solution.py:62
  49.5 8.6 %copy-start.9 = (bf16[64,512]{1,0:T(8,128)(2,1)S(1)}, bf16[64,512]{1,0:T(8,128)(2,1)}, u32[]{:S(2)}) copy-start(bf16[64,512]{1,0:T(8,128)(2,1)} %param.14) | copy-start | bytes 196612
  67.0 212.5 %all-reduce.6.cloned.1.call-start = ((), (), s32[]{:S(2)}) async-start(), calls=%async_computation.1 | async-start | bytes 4194304 | tf_op jit(solution)/shard_map/psum | solution.py:69
  168.9 2.5 copy-start.2
  168.9 3.7 %copy-start.7 = (bf16[512,256]{1,0:T(8,128)(2,1)S(1)}, bf16[512,256]{1,0:T(8,128)(2,1)}, u32[]{:S(2)}) copy-start(bf16[512,256]{1,0:T(8,128)(2,1)} %param.15) | copy-start | bytes 786436
  172.6 5.2 %copy-start.5 = (bf16[256,128]{1,0:T(8,128)(2,1)S(1)}, bf16[256,128]{1,0:T(8,128)(2,1)}, u32[]{:S(2)}) copy-start(bf16[256,128]{1,0:T(8,128)(2,1)} %param.12) | copy-start | bytes 196612
  172.6 5.2 %copy-start.6 = (f32[1,256]{1,0:T(1,128)S(1)}, f32[1,256]{1,0:T(1,128)}, u32[]{:S(2)}) copy-start(f32[1,256]{1,0:T(1,128)} %param.10) | copy-start | bytes 3076
  177.8 127.3 %all-reduce.8.cloned.1.call-start = ((), (), s32[]{:S(2)}) async-start(), calls=%async_computation.2 | async-start | bytes 524288 | tf_op jit(solution)/shard_map/psum | solution.py:78
  279.5 3.6 %copy-start.3 = (bf16[2048,512]{1,0:T(8,128)(2,1)S(1)}, bf16[2048,512]{1,0:T(8,128)(2,1)}, u32[]{:S(2)}) copy-start(bf16[2048,512]{1,0:T(8,128)(2,1)} %all-reduce.4.cloned.1.call-done) | copy-start | bytes 6291460
  279.5 3.6 %copy-start.4 = (bf16[2048,512]{1,0:T(8,128)(2,1)S(1)}, bf16[2048,512]{1,0:T(8,128)(2,1)}, u32[]{:S(2)}) copy-start(bf16[2048,512]{1,0:T(8,128)(2,1)} %all-reduce.6.cloned.1.call-done) | copy-start | bytes 6291460
  283.1 1.7 copy-start.10
Sparse Core Ops, SparseCore 0:
  67.2 101.6 all-reduce.3
  177.9 101.5 all-reduce.5
  287.5 17.5 all-reduce.7
where the time goes:
time: 314 us; the launch traced here: 313 us
  waiting for transfers between devices  202 us (64%)
  blocking collectives  47.1 us (15%)
  matrix products  27.4 us (9%)
  other arithmetic  23.7 us (8%)
  between operations  13.3 us (4%)
    psum x1, waiting for transfers between devices, local(): lax.psum(jnp.dot(head_out, out_weight, preferred_element_type=jnp.float32...  102 us
    psum x1, waiting for transfers between devices, local(): lax.psum(jnp.dot(hidden, down_weight, preferred_element_type=jnp.float32)...  82.3 us
    all_gather x1, blocking collectives, local(): lax.all_gather(block_local, 'tp', axis=0, tiled=True)  27.8 us
    all_gather x1, blocking collectives, local(): lax.all_gather(final_local, 'tp', axis=0, tiled=True)  19.2 us
    psum x1, waiting for transfers between devices, local(): lax.psum((weighting * predicted).astype(jnp.bfloat16), 'cfg')  17.7 us
    dot_general x1, matrix products, local(): jnp.dot(head_out, out_weight, preferred_element_type=jnp.float32)  8.92 us
    reduce_sum x1, other arithmetic, attend(): softmaxed = jax.nn.softmax(scores, axis=-1)  8.58 us
    dot_general x1, matrix products, attend(): jnp.einsum('thd,shd->hts', per_head[:, 0], per_head[:, 1], preferred_elem...  8.09 us
  transfers between devices with their start and end apart: 3, of which 3 were waited for; matrix products, arithmetic and copies ran while one was open for 0% of the time, Pallas kernels for 0%

commit v1 on v0

--- a/solution.py
+++ b/solution.py
@@ -1,3 +1,4 @@
+import functools
 import jax
 import jax.numpy as jnp
 from jax import lax
@@ -6,6 +7,13 @@
 HEAD_SIZE = 64
 guidance = 4.0
 epsilon = 1e-06
+
+
+def name_scales(x0, mesh_ax):
+    return jnp.sum(lax.all_gather(x0, mesh_ax), 0)
+
+
+enter_the_regions = functools.partial(name_scales, mesh_ax="tp")
 
 
 def layer_norm(values):
@@ -59,8 +67,8 @@
         "td,dke->tke", normed, qkv_weight, preferred_element_type=jnp.float32
     ).astype(jnp.bfloat16)
     head_out = attend(projected)
-    attended = lax.psum(
-        jnp.dot(head_out, out_weight, preferred_element_type=jnp.float32).astype(jnp.bfloat16), "tp"
+    attended = enter_the_regions(
+        jnp.dot(head_out, out_weight, preferred_element_type=jnp.float32).astype(jnp.bfloat16)
     ).astype(jnp.float32)
     stream = stream + shifts[2] * attended
     normed = modulate(stream, shifts[4], shifts[3])

time: 314 us -> 448 us (1.43)
  waiting for transfers between devices: 202 us -> 327 us
  other arithmetic: 23.7 us -> 34.2 us
    all_gather x0 -> x1, waiting for transfers between devices: none -> 227 us  [name_scales(): return jnp.sum(lax.all_gather(x0, mesh_ax), 0)]
    psum x1 -> x0, waiting for transfers between devices: 102 us -> none  [local(): lax.psum(jnp.dot(head_out, out_weight, preferred_element_type=jnp.float32...]
    reduce_sum x0 -> x1, other arithmetic: none -> 10.5 us  [name_scales(): return jnp.sum(lax.all_gather(x0, mesh_ax), 0)]
where the time goes in v1:
time: 448 us
  waiting for transfers between devices  327 us (73%)
  blocking collectives  46 us (10%)
  other arithmetic  34.2 us (8%)
  matrix products  27.3 us (6%)
  between operations  13.3 us (3%)
    all_gather x1, waiting for transfers between devices, name_scales(): return jnp.sum(lax.all_gather(x0, mesh_ax), 0)  227 us
    psum x1, waiting for transfers between devices, local(): lax.psum(jnp.dot(hidden, down_weight, preferred_element_type=jnp.float32)...  82.3 us
    all_gather x1, blocking collectives, local(): lax.all_gather(block_local, 'tp', axis=0, tiled=True)  27.8 us
    all_gather x1, blocking collectives, local(): lax.all_gather(final_local, 'tp', axis=0, tiled=True)  18.1 us
    psum x1, waiting for transfers between devices, local(): lax.psum((weighting * predicted).astype(jnp.bfloat16), 'cfg')  17.7 us
    reduce_sum x1, other arithmetic, name_scales(): return jnp.sum(lax.all_gather(x0, mesh_ax), 0)  10.5 us
  transfers between devices with their start and end apart: 3, of which 3 were waited for; matrix products, arithmetic and copies ran while one was open for 0% of the time, Pallas kernels for 0%

profile of v1, /device:TPU:0, one launch (start us, length us, event | category | flops | bytes accessed | tf_op | source)
XLA Modules:
  0.0 447.8 jit_solution(7541108120411694951)
XLA Ops:
  6.5 0.0 copy-start
  6.5 0.0 copy-start.1
  6.5 0.0 copy-start.8
  6.5 0.0 all-gather.5.cloned.1.call-start
  6.5 1.2 convolution_bitcast_fusion
  7.8 27.8 %all-gather.1 = f32[8,1,384]{2,1,0:T(1,128)S(1)} all-gather(f32[1,1,384]{2,1,0:T(1,128)S(1)} %convolution_bitcast_fusion), channel_id=1, replica_groups=mesh['cfg'=2,'tp'=8,'dp'=2] {'tp'}, dimensions={0}, use_global_device_ids=true | all-gather | bytes 13824 | tf_op jit(solution)/shard_map/all_gather | solution.py:60
  35.6 1.9 convert_reduce_fusion
  37.6 2.5 fusion.8
  40.1 0.0 copy-done.1
  40.1 0.0 copy-done.8
  40.1 1.2 fusion.28
  41.3 0.1 convert_bitcast_fusion
  41.4 8.1 %multiply_reduce_fusion = (f32[2048]{0:T(1024)S(1)}, f32[2048,2048]{0,1:T(8,128)}) fusion(bf16[2048,3,1,64]{0,3,1,2:T(8,128)(2,1)S(1)} %convert_bitcast_fusion), kind=kOutput, calls=%fused_computation.3 | convolution fusion | flops 545257472 | bytes 17309696 | tf_op jit(solution)/shard_map/thd,shd->hts/dot_general | solution.py:35
  49.5 0.0 copy-start.9
  49.5 8.6 %fusion.2 = f32[2048]{0:T(1024)S(1)} fusion(f32[2048,2048]{0,1:T(8,128)} %get-tuple-element.14, f32[2048]{0:T(1024)S(1)} %get-tuple-element.13), kind=kLoop, calls=%fused_computation.4 | loop fusion | flops 12580864 | bytes 16793600 | tf_op jit(solution)/shard_map/reduce_sum | solution.py:38
  58.1 0.0 copy-done.9
  58.1 8.9 %convolution_convert_fusion.1 = bf16[2048,512]{1,0:T(8,128)(2,1)} fusion(bf16[64,512]{1,0:T(8,128)(2,1)S(1)} %copy-done.9, f32[2048,2048]{0,1:T(8,128)} %get-tuple-element.14, f32[2048]{0:T(1024)S(1)} %fusion.2, f32[2048]{0:T(1024)S(1)} %get-tuple-element.13, bf16[2048,3,1,64]{0,3,1,2:T(8,128)(2,1)S(1)} %convert_bitcast_fusion), kind=kOutput, calls=%fused_computation.24 | convolution fusion | flops 684851200 | bytes 19218432 | tf_op jit(solution)/shard_map/dot_general | solution.py:71
  67.0 0.0 all-gather.5.cloned.1.call-update
  67.0 0.2 all-reduce.3.cloned.1.call-start
  67.3 226.6 %all-gather.5.cloned.1.call-done = bf16[16384,512]{1,0:T(8,128)(2,1)} async-done(((bf16[2048,512]{1,0:T(8,128)(2,1)}), bf16[16384,512]{1,0:T(8,128)(2,1)}) %all-gather.5.cloned.1.call-update) | async-done | bytes 16777232 | tf_op jit(solution)/shard_map/all_gather | solution.py:13
  293.9 10.5 %reduce_sum.78 = bf16[2048,512]{1,0:T(8,128)(2,1)} reduce(bf16[8,2048,512]{2,1,0:T(8,128)(2,1)} %bitcast.48, bf16[]{:T(256)} %constant.38.clone.1), dimensions={0}, to_apply=%region_4.5 | reduce | flops 7340032 | bytes 18874370 | tf_op jit(solution)/shard_map/reduce_sum | solution.py:13
  304.4 0.0 copy-start.2
  304.4 0.0 copy-start.7
  304.4 2.5 fusion.12
  306.9 0.0 copy-done.2
  307.0 1.2 multiply_reduce_fusion.2
  308.1 0.0 copy-done
  308.2 0.0 copy-done.7
  308.2 0.0 copy-start.5
  308.2 0.0 copy-start.6
  308.2 5.1 %convolution_convert_fusion = bf16[2048,512]{1,0:T(8,128)(2,1)} fusion(bf16[256,512]{1,0:T(8,128)(2,1)S(1)} %copy-done, bf16[512,256]{1,0:T(8,128)(2,1)S(1)} %copy-done.7, bf16[2048,512]{1,0:T(8,128)(2,1)} %reduce_sum.78, bf16[2048,512]{1,0:T(8,128)(2,1)S(1)} %copy-done.1, f32[512]{0:T(512)S(1)} %get-tuple-element.6, f32[512]{0:T(512)S(1)} %get-tuple-element.7, ...), kind=kOutput, calls=%fused_computation.23 | convolution fusion | flops 1088946176 | bytes 6838272 | tf_op jit(solution)/shard_map/dot_general | solution.py:78
  313.3 0.0 all-reduce.3.cloned.1.call-update
  313.3 0.0 all-reduce.5.cloned.1.call-start
  313.3 0.0 copy-done.5
  313.3 0.0 copy-done.6
  313.4 0.1 convolution_bitcast_fusion.1
  313.5 18.1 %all-gather.2 = f32[8,1,128]{2,1,0:T(1,128)S(1)} all-gather(f32[1,1,128]{2,1,0:T(1,128)S(1)} %convolution_bitcast_fusion.1), channel_id=1, replica_groups=mesh['cfg'=2,'tp'=8,'dp'=2] {'tp'}, dimensions={0}, use_global_device_ids=true | all-gather | bytes 4608 | tf_op jit(solution)/shard_map/all_gather | solution.py:61
  331.6 82.3 %all-reduce.3.cloned.1.call-done = bf16[2048,512]{1,0:T(8,128)(2,1)} async-done(((bf16[2048,512]{1,0:T(8,128)(2,1)}), bf16[2048,512]{1,0:T(8,128)(2,1)}) %all-reduce.3.cloned.1.call-update) | async-done | bytes 2097168 | tf_op jit(solution)/shard_map/psum | solution.py:77
  413.9 3.5 fusion.45
  417.4 0.0 copy-start.10
  417.5 0.0 copy-done.3
  417.5 0.0 copy-done.4
  417.5 1.6 multiply_reduce_fusion.1
  419.1 0.0 copy-done.10
  419.1 2.7 fusion.13
  421.8 0.0 all-reduce.5.cloned.1.call-update
  421.8 17.7 %all-reduce.5.cloned.1.call-done = bf16[2048,64]{0,1:T(8,128)(2,1)} async-done(((bf16[2048,64]{0,1:T(8,128)(2,1)}), bf16[2048,64]{0,1:T(8,128)(2,1)}) %all-reduce.5.cloned.1.call-update) | async-done | bytes 262160 | tf_op jit(solution)/shard_map/psum | solution.py:86
  439.5 1.8 convert_element_type.70
  (10 shorter events, 0.0 us)
Async XLA Ops:
  6.5 301.6 %copy-start = (bf16[256,512]{1,0:T(8,128)(2,1)S(1)}, bf16[256,512]{1,0:T(8,128)(2,1)}, u32[]{:S(2)}) copy-start(bf16[256,512]{1,0:T(8,128)(2,1)} %param.16) | copy-start | bytes 786436
  6.5 33.5 %copy-start.1 = (bf16[2048,512]{1,0:T(8,128)(2,1)S(1)}, bf16[2048,512]{1,0:T(8,128)(2,1)}, u32[]{:S(2)}) copy-start(bf16[2048,512]{1,0:T(8,128)(2,1)} %param.9) | copy-start | bytes 6291460
  6.5 33.6 %copy-start.8 = (bf16[512,3,64]{0,2,1:T(8,128)(2,1)S(1)}, bf16[512,3,64]{0,2,1:T(8,128)(2,1)}, u32[]{:S(2)}) copy-start(bf16[512,3,64]{0,2,1:T(8,128)(2,1)} %param.13) | copy-start | bytes 589828
  6.5 287.3 %all-gather.5.cloned.1.call-start = ((), (), s32[]{:S(2)}) async-start(), calls=%async_computation.2 | async-start | bytes 18874368 | tf_op jit(solution)/shard_map/all_gather | solution.py:13
  49.5 8.6 %copy-start.9 = (bf16[64,512]{1,0:T(8,128)(2,1)S(1)}, bf16[64,512]{1,0:T(8,128)(2,1)}, u32[]{:S(2)}) copy-start(bf16[64,512]{1,0:T(8,128)(2,1)} %param.14) | copy-start | bytes 196612
  67.0 346.9 %all-reduce.3.cloned.1.call-start = ((), (), s32[]{:S(2)}) async-start(), calls=%async_computation | async-start | bytes 4194304 | tf_op jit(solution)/shard_map/psum | solution.py:77
  304.4 2.5 copy-start.2
  304.4 3.7 copy-start.7
  308.2 5.2 %copy-start.5 = (bf16[256,128]{1,0:T(8,128)(2,1)S(1)}, bf16[256,128]{1,0:T(8,128)(2,1)}, u32[]{:S(2)}) copy-start(bf16[256,128]{1,0:T(8,128)(2,1)} %param.12) | copy-start | bytes 196612
  308.2 5.2 %copy-start.6 = (f32[1,256]{1,0:T(1,128)S(1)}, f32[1,256]{1,0:T(1,128)}, u32[]{:S(2)}) copy-start(f32[1,256]{1,0:T(1,128)} %param.10) | copy-start | bytes 3076
  313.3 126.2 %all-reduce.5.cloned.1.call-start = ((), (), s32[]{:S(2)}) async-start(), calls=%async_computation.1 | async-start | bytes 524288 | tf_op jit(solution)/shard_map/psum | solution.py:86
  413.9 3.6 copy-start.3
  413.9 3.6 copy-start.4
  417.4 1.7 copy-start.10
Sparse Core Ops, SparseCore 0:
  67.2 226.6 all-gather.4
  313.4 100.4 all-reduce.2
  421.9 17.5 all-reduce.4
